TPU v7x, 32 devices: a whole 2x2x4 slice. The times are simulated.
32 devices in a mesh: crop: 1, row: 32 (over z, y, x, core).
Axes of the slice: x: 2, y: 2, z: 4, core: 2. Of those that a mesh axis runs over, the one named last changes fastest.
Arguments:
- queries: bfloat16 [128, 128, 128], P(('crop', 'row')), may hold values from -4 to 4
- keys: bfloat16 [128, 128, 128], P(('crop', 'row')), may hold values from -4 to 4
- values: bfloat16 [128, 128, 128], P(('crop', 'row')), may hold values from -6 to 6
- grads_out: bfloat16 [128, 128, 128], P(('crop', 'row')), may hold values from -96 to 96
- log_norm: float32 [128, 4, 128], P(('crop', 'row')), may hold values from -90 to 102, as said below
- bias: bfloat16 [128, 4, 128], P(('crop', 'row')), may hold values from -4 to 4
Outputs:
- query_grad: bfloat16 [128, 128, 128], P(('crop', 'row'))
- key_grad: bfloat16 [128, 128, 128], P(('crop', 'row'))
- value_grad: bfloat16 [128, 128, 128], P(('crop', 'row'))
- bias_grad: float32 [128, 4, 128], P(('crop', 'row'))
Inputs may be any that keep to these rules, and one draw needn't show every extreme that they name: log_norm[i, h, j] is the logarithm of the sum over k of exp(scores[i, h, j, k]), scores computed from the given queries, keys and bias.
All inputs are finite; a program needn't handle non-finite values.
Results may differ from a plain program's by a relative error of at most 0.0051.
Values may be sent and summed in bfloat16 or wider, within the bound.
A program may use at most 64 MiB of HBM per device.

v0:
```python
import math

import jax
import jax.numpy as jnp
from jax import lax
from jax.sharding import PartitionSpec as P


def block_terms(arrays, bias_rows, first_row):
    queries, keys, values, grads_out, log_norm, head_count = arrays
    local_rows, length, pair_width = queries.shape
    head_width = pair_width // head_count
    row_count = bias_rows.shape[0]
    score_scale = head_width ** (-0.5)
    query_block = lax.dynamic_slice_in_dim(queries, first_row, row_count, 1).reshape(
        local_rows, row_count, head_count, head_width
    )
    grad_block = lax.dynamic_slice_in_dim(grads_out, first_row, row_count, 1).reshape(
        local_rows, row_count, head_count, head_width
    )
    key_heads = keys.reshape(local_rows, length, head_count, head_width)
    value_heads = values.reshape(local_rows, length, head_count, head_width)
    norm_block = lax.dynamic_slice_in_dim(log_norm, first_row, row_count, 2)
    scores = (
        jnp.einsum("rjhd,rkhd->rhjk", query_block, key_heads, preferred_element_type=jnp.float32)
        * score_scale
    )
    scores = scores + jnp.transpose(bias_rows, (1, 0, 2))[None].astype(jnp.float32)
    weights = jnp.exp(scores - norm_block[..., None])
    weight_grads = jnp.einsum(
        "rjhd,rkhd->rhjk", grad_block, value_heads, preferred_element_type=jnp.float32
    )
    centre = jnp.sum(weights * weight_grads, axis=-1, keepdims=True)
    score_grads = weights * (weight_grads - centre)
    return (query_block, grad_block, key_heads, weights, score_grads, score_scale)


def block_grads(arrays, bias_rows, first_row):
    query_block, grad_block, key_heads, weights, score_grads, score_scale = block_terms(
        arrays, bias_rows, first_row
    )
    local_rows, row_count, head_count, head_width = query_block.shape
    length = key_heads.shape[1]
    weights_low = weights.astype(jnp.bfloat16)
    grads_low = score_grads.astype(jnp.bfloat16)
    query_part = (
        jnp.einsum("rhjk,rkhd->rjhd", grads_low, key_heads, preferred_element_type=jnp.float32)
        * score_scale
    )
    key_part = (
        jnp.einsum("rhjk,rjhd->rkhd", grads_low, query_block, preferred_element_type=jnp.float32)
        * score_scale
    )
    value_part = jnp.einsum(
        "rhjk,rjhd->rkhd", weights_low, grad_block, preferred_element_type=jnp.float32
    )
    bias_part = jnp.transpose(jnp.sum(score_grads, axis=0), (1, 0, 2))
    pair_width = head_count * head_width
    return (
        query_part.reshape(local_rows, row_count, pair_width),
        key_part.reshape(local_rows, length, pair_width),
        value_part.reshape(local_rows, length, pair_width),
        bias_part,
    )


def sweep(arrays, bias_rows, running):
    total_rows = bias_rows.shape[0]
    block_rows = math.gcd(total_rows, 64)

    def sweep_advance(block_index, state):
        offset = block_index * block_rows
        rows_now = lax.dynamic_slice_in_dim(bias_rows, offset, block_rows, 0)
        query_part, key_part, value_part, bias_part = block_grads(arrays, rows_now, offset)
        query_sum, key_sum, value_sum, bias_sum = state
        query_sum = lax.dynamic_update_slice_in_dim(query_sum, query_part, offset, 1)
        key_sum = key_sum + key_part
        value_sum = value_sum + value_part
        return (query_sum, key_sum, value_sum, bias_sum)

    return lax.fori_loop(0, total_rows // block_rows, sweep_advance, running)


def gather_bias(bias):
    return lax.all_gather(bias, "row", axis=0, tiled=True)


def local(queries, keys, values, grads_out, log_norm, bias):
    head_count = bias.shape[1]
    local_rows, length, pair_width = queries.shape
    arrays = (queries, keys, values, grads_out, log_norm, head_count)
    blank = jnp.zeros((local_rows, length, pair_width), jnp.float32)
    gathered = gather_bias(bias)
    query_sum, key_sum, value_sum, unused = sweep(arrays, gathered, (blank, blank, blank, None))
    row_count = local_rows * lax.axis_size("row")
    block_rows = math.gcd(row_count, 64)

    def bias_advance(block_index, total):
        offset = block_index * block_rows
        rows_now = lax.dynamic_slice_in_dim(gathered, offset, block_rows, 0)
        score_grads = block_terms(arrays, rows_now, offset)[4]
        bias_part = jnp.transpose(jnp.sum(score_grads, axis=0), (1, 0, 2))
        return lax.dynamic_update_slice_in_dim(total, bias_part, offset, 0)

    start_total = jnp.zeros((row_count, head_count, length), jnp.float32)
    bias_grad = lax.psum_scatter(
        lax.fori_loop(0, row_count // block_rows, bias_advance, start_total),
        "row",
        scatter_dimension=0,
        tiled=True,
    )
    return (
        query_sum.astype(jnp.bfloat16),
        key_sum.astype(jnp.bfloat16),
        value_sum.astype(jnp.bfloat16),
        bias_grad,
    )


def solution(mesh):
    placed = (
        P(("crop", "row"), None, None),
        P(("crop", "row"), None, None),
        P(("crop", "row"), None, None),
        P(("crop", "row"), None, None),
        P(("crop", "row"), None, None),
        P(("crop", "row"), None, None),
    )
    return jax.shard_map(
        local,
        mesh=mesh,
        in_specs=placed,
        out_specs=(
            P(("crop", "row"), None, None),
            P(("crop", "row"), None, None),
            P(("crop", "row"), None, None),
            P(("crop", "row"), None, None),
        ),
        check_vma=False,
    )
```

profile of v0, /device:TPU:0, one launch (start us, length us, event | category | flops | bytes accessed | tf_op | source)
XLA Modules:
  0.0 189.5 jit_solution(9445011809489944761)
XLA Ops:
  7.2 43.9 %all_gather.3 = bf16[128,4,128]{2,1,0:T(4,128)(2,1)S(1)} all-gather(bf16[4,4,128]{2,1,0:T(4,128)(2,1)} %param.15), channel_id=1, replica_groups=mesh['crop'=1,'row'=32] {'row'}, dimensions={0}, use_global_device_ids=true | all-gather | bytes 135168 | tf_op jit(solution)/shard_map/all_gather | solution.py:85
  51.1 0.9 copy-done.2
  52.1 0.8 copy-done.3
  53.0 0.8 copy-done.4
  53.9 0.8 copy-done.5
  54.9 0.6 copy-done.1
  55.5 2.3 %while.31 = (s32[]{:T(128)}, f32[128,4,128]{2,1,0:T(4,128)S(1)}, bf16[4,128,128]{1,2,0:T(8,128)(2,1)S(1)}, bf16[4,128,128]{1,2,0:T(8,128)(2,1)S(1)}, bf16[128,4,...) while((s32[]{:T(128)}, f32[128,4,128]{2,1,0:T(4,128)S(1)}, ...), condition=%wide.region_6.0_spmd, body=%wide.region_3.0_spmd.sunk | while | flops 26084484 | bytes 2437299 | solution.py:107
  55.8 0.3 fusion.57
  56.1 0.4 fusion.58
  56.7 0.1 constant_dynamic-slice_fusion.12
  56.9 0.3 fusion.57
  57.3 0.4 fusion.58
  57.8 0.7 copy-done
  58.6 4.6 %while.32 = (s32[]{:T(128)}, bf16[4,128,128]{2,1,0:T(8,128)(2,1)S(1)}, f32[4,128,128]{1,2,0:T(8,128)S(1)}, f32[4,128,128]{1,2,0:T(8,128)S(1)}, bf16[4,128,128]{1...) while((s32[]{:T(128)}, ...), condition=%wide.region_2.0_spmd.clone, body=%wide.region_0.0_spmd.clone.sunk | while | flops 43547652 | bytes 7622865 | solution.py:81
  58.7 0.3 fusion.69
  59.2 0.5 multiply_reduce_fusion.3
  59.7 0.2 multiply_convert_fusion.2
  59.9 0.2 convolution_multiply_fusion.7
  60.1 0.2 fusion.70
  60.3 0.1 bitcast_add_fusion.3
  60.5 0.2 convolution_multiply_fusion.6
  61.0 0.3 fusion.69
  61.5 0.5 multiply_reduce_fusion.3
  62.0 0.2 multiply_convert_fusion.2
  62.2 0.2 convolution_multiply_fusion.7
  62.4 0.2 fusion.70
  62.6 0.1 bitcast_add_fusion.3
  62.7 0.2 convolution_multiply_fusion.6
  63.2 0.8 copy.28
  63.9 0.8 copy.29
  64.7 116.7 %all-reduce.3.cloned.1.call-done = f32[128,4,128]{2,1,0:T(4,128)} async-done(((f32[128,4,128]{2,1,0:T(4,128)}), f32[128,4,128]{2,1,0:T(4,128)}) %all-reduce.3.cloned.1.call-update) | async-done | bytes 262160
  181.4 1.3 constant_dynamic-slice_fusion.6
  (38 shorter events, 2.1 us)
Async XLA Ops:
  7.2 174.2 %all-reduce.3.cloned.1.call-start = ((), (), s32[]{:S(2)}) async-start(), calls=%async_computation | async-start | bytes 524288
  51.1 0.9 copy-start.2
  52.0 0.9 copy-start.3
  52.9 0.9 copy-start.4
  53.8 0.9 copy-start.5
  54.8 0.7 copy-start.1
  57.8 0.7 copy-start
  63.1 0.8 copy-start.6
Sparse Core Ops, SparseCore 0:
  58.7 122.6 all-reduce.2
where the time goes:
time: 190 us
  waiting for transfers between devices  117 us (62%)
  blocking collectives  43.9 us (23%)
  between operations  14.1 us (7%)
  local copies, waits for them, and re-layouts  9.41 us (5%)
  matrix products  4.34 us (2%)
    unnamed x2, waiting for transfers between devices  117 us
    all_gather x1, blocking collectives, gather_bias(): return lax.all_gather(bias, 'row', axis=0, tiled=True)  43.9 us
    unnamed x20, local copies, waits for them, and re-layouts  6.37 us
  transfers between devices with their start and end apart: 1, of which 1 were waited for; matrix products, arithmetic and copies ran while one was open for 3% of the time, Pallas kernels for 0%

commit v1 on v0

v1 whole, which is shorter than its diff:
```python
import functools
import math

import jax
import jax.numpy as jnp
from jax import lax
from jax.experimental import pallas as pl
from jax.experimental.pallas import tpu as pltpu
from jax.sharding import PartitionSpec as P

F32 = jnp.float32
BF16 = jnp.bfloat16


def peers(me, count, body):
    def step(d, carry):
        body(d, lax.rem(me + d, count))
        return carry

    lax.fori_loop(1, count, step, 0)


def kernel(
    count, heads,
    q_hbm, k_hbm, v_hbm, g_hbm, norm_hbm, bias_hbm,
    qg_ref, kg_ref, vg_ref, bg_ref,
    q, k, v, g, norm, gath, qm, gm, kt, e1, dp, eb, p_low, s_low, wide, terms, landed,
    in_sem, gath_send, gath_recv, term_send, term_recv,
):
    me = lax.axis_index("row")
    rows, length, channels = q.shape
    width = channels // heads
    block = bias_hbm.shape[0]
    lanes = wide.shape[2]
    scale = width ** (-0.5)
    own = pl.ds(pl.multiple_of(me * block, block), block)

    barrier = pltpu.get_barrier_semaphore()
    peers(me, count, lambda d, t: pl.semaphore_signal(barrier, inc=1, device_id={"row": t}))

    pairs = ((bias_hbm, gath.at[own]), (q_hbm, q), (k_hbm, k), (v_hbm, v), (g_hbm, g), (norm_hbm, norm))
    copies = [pltpu.make_async_copy(a, b, in_sem.at[i]) for i, (a, b) in enumerate(pairs)]
    for copy in copies:
        copy.start()
    copies[0].wait()
    pl.semaphore_wait(barrier, count - 1)

    def gather_copy(t):
        return pltpu.make_async_remote_copy(
            src_ref=gath.at[own], dst_ref=gath.at[own], send_sem=gath_send, recv_sem=gath_recv,
            device_id={"row": t},
        )

    peers(me, count, lambda d, t: gather_copy(t).start())

    for copy in copies[1:]:
        copy.wait()
    channel = lax.broadcasted_iota(jnp.int32, (1, channels), 1)
    masks = [
        jnp.where((channel >= h * width) & (channel < (h + 1) * width), 1.0, 0.0).astype(BF16)
        for h in range(heads)
    ]
    nt = (((1,), (1,)), ((), ()))
    for i in range(rows):
        for h in range(heads):
            span = pl.ds(h * length, length)
            qm[i, span, :] = q[i] * masks[h]
            gm[i, span, :] = g[i] * masks[h]
        kt[i] = k[i].astype(F32).T.astype(BF16)
        score = lax.dot_general(k[i], qm[i], nt, preferred_element_type=F32)
        grad = lax.dot_general(v[i], gm[i], nt, preferred_element_type=F32)
        dp[i] = grad
        for h in range(heads):
            line = norm[pl.ds(i * heads + h, 1), :]
            tile = score[:, h * length:(h + 1) * length]
            e1[i, :, pl.ds(h * length, length)] = jnp.exp(tile * scale - line)

    others = pl.ds(0, (count - 1) * block)
    pltpu.make_async_copy(gath.at[others], gath.at[others], gath_recv).wait()

    for c in range(length // lanes):
        column = pl.ds(c * lanes, lanes)
        wide[c] = jnp.exp(gath[:, column].astype(F32))
        for h in range(heads):
            eb[h, column, :] = wide[c, pl.ds(h, length, stride=heads), :].T

    for h in range(heads):
        span = pl.ds(h * length, length)
        total = None
        for i in range(rows):
            weights = e1[i, :, span] * eb[h]
            grad = dp[i, :, span]
            centre = jnp.sum(weights * grad, axis=0, keepdims=True)
            score_grads = weights * (grad - centre)
            p_low[i, :, span] = weights.astype(BF16)
            s_low[i, :, span] = score_grads.astype(BF16)
            total = score_grads if total is None else total + score_grads
        for c in range(length // lanes):
            wide[c, pl.ds(h, length, stride=heads), :] = total[c * lanes:(c + 1) * lanes, :].T
    for c in range(length // lanes):
        terms[:, pl.ds(c * lanes, lanes)] = wide[c].astype(BF16)

    def term_copy(d, t):
        theirs = pl.ds(pl.multiple_of(t * block, block), block)
        return pltpu.make_async_remote_copy(
            src_ref=terms.at[theirs], dst_ref=landed.at[d], send_sem=term_send, recv_sem=term_recv,
            device_id={"row": t},
        )

    peers(me, count, lambda d, t: term_copy(d, t).start())

    for i in range(rows):
        key_part = jnp.dot(s_low[i], qm[i], preferred_element_type=F32)
        kg_ref[i] = (key_part * scale).astype(BF16)
        vg_ref[i] = jnp.dot(p_low[i], gm[i], preferred_element_type=F32).astype(BF16)
        parts = [
            jnp.dot(
                kt[i, pl.ds(h * width, width), :], s_low[i, :, pl.ds(h * length, length)],
                preferred_element_type=F32,
            )
            for h in range(heads)
        ]
        qg_ref[i] = (jnp.concatenate(parts, axis=0).T * scale).astype(BF16)

    arrived = landed.at[pl.ds(1, count - 1)]
    pltpu.make_async_copy(arrived, arrived, term_recv).wait()
    for c in range(length // lanes):
        column = pl.ds(c * lanes, lanes)
        got = jnp.sum(landed[pl.ds(1, count - 1), :, column].astype(F32), axis=0)
        bg_ref[:, column] = wide[c, own, :] + got
    pltpu.make_async_copy(gath.at[others], gath.at[others], gath_send).wait()
    pltpu.make_async_copy(arrived, arrived, term_send).wait()


def local(count, queries, keys, values, grads_out, log_norm, bias):
    rows, length, channels = queries.shape
    bias_rows, heads, _ = bias.shape
    block = bias_rows * heads
    lanes = math.gcd(length, 128)
    any_space = pl.BlockSpec(memory_space=pl.ANY)
    vmem = pl.BlockSpec(memory_space=pltpu.VMEM)
    big = (rows, length, channels)
    outs = pl.pallas_call(
        functools.partial(kernel, count, heads),
        out_shape=(
            jax.ShapeDtypeStruct(big, BF16),
            jax.ShapeDtypeStruct(big, BF16),
            jax.ShapeDtypeStruct(big, BF16),
            jax.ShapeDtypeStruct((block, length), F32),
        ),
        in_specs=[any_space] * 6,
        out_specs=(vmem,) * 4,
        scratch_shapes=[
            pltpu.VMEM(big, BF16),
            pltpu.VMEM(big, BF16),
            pltpu.VMEM(big, BF16),
            pltpu.VMEM(big, BF16),
            pltpu.VMEM((rows * heads, length), F32),
            pltpu.VMEM((count * block, length), BF16),
            pltpu.VMEM((rows, heads * length, channels), BF16),
            pltpu.VMEM((rows, heads * length, channels), BF16),
            pltpu.VMEM((rows, channels, length), BF16),
            pltpu.VMEM((rows, length, heads * length), F32),
            pltpu.VMEM((rows, length, heads * length), F32),
            pltpu.VMEM((heads, length, length), F32),
            pltpu.VMEM((rows, length, heads * length), BF16),
            pltpu.VMEM((rows, length, heads * length), BF16),
            pltpu.VMEM((length // lanes, length * heads, lanes), F32),
            pltpu.VMEM((count * block, length), BF16),
            pltpu.VMEM((count, block, length), BF16),
            pltpu.SemaphoreType.DMA((6,)),
            pltpu.SemaphoreType.DMA,
            pltpu.SemaphoreType.DMA,
            pltpu.SemaphoreType.DMA,
            pltpu.SemaphoreType.DMA,
        ],
        compiler_params=pltpu.CompilerParams(collective_id=0, has_side_effects=True),
    )(
        queries, keys, values, grads_out,
        log_norm.reshape(rows * heads, length), bias.reshape(block, length),
    )
    return outs[0], outs[1], outs[2], outs[3].reshape(bias_rows, heads, length)


def solution(mesh):
    placed = P(("crop", "row"), None, None)
    return jax.shard_map(
        functools.partial(local, mesh.shape["row"]),
        mesh=mesh,
        in_specs=(placed,) * 6,
        out_specs=(placed,) * 4,
        check_vma=False,
    )
```

time: 190 us -> 23.5 us (0.12)
  waiting for transfers between devices: 117 us -> 0 us
  blocking collectives: 43.9 us -> 0 us
  Pallas kernels: 0 us -> 18.7 us
  between operations: 14.1 us -> 0.65 us
  local copies, waits for them, and re-layouts: 9.41 us -> 3.85 us
  matrix products: 4.34 us -> 0 us
    unnamed x2 -> x0, waiting for transfers between devices: 117 us -> none
    all_gather x1 -> x0, blocking collectives: 43.9 us -> none  [gather_bias(): return lax.all_gather(bias, 'row', axis=0, tiled=True)]
    pallas_call x0 -> x1, Pallas kernels: none -> 18.7 us  [local(): pl.pallas_call(functools.partial(kernel, count, heads), out_shape=(jax.Sh...]
    dot_general x12 -> x0, matrix products: 3.47 us -> none  [the longest x4 1.68 us: block_terms(): jnp.einsum('rjhd,rkhd->rhjk', query_block, key_heads, preferred_element_t...]
    unnamed x20 -> x10, local copies, waits for them, and re-layouts: 6.37 us -> 3.85 us
  transfers between devices with their start and end apart: 1 -> 0, of which waited for: 1 -> 0; matrix products, arithmetic and copies ran while one was open for 3% -> 0% of each run, Pallas kernels for 0% -> 0%
where the time goes in v1:
time: 23.5 us; the launch traced here: 23.3 us
  Pallas kernels  18.7 us (80%)
  local copies, waits for them, and re-layouts  3.85 us (16%)
  between operations  0.65 us (3%)
    pallas_call x1, Pallas kernels, local(): pl.pallas_call(functools.partial(kernel, count, heads), out_shape=(jax.Sh...  18.7 us
    unnamed x10, local copies, waits for them, and re-layouts  3.85 us

profile of v1, /device:TPU:0, one launch (start us, length us, event | category | flops | bytes accessed | tf_op | source)
XLA Modules:
  0.0 23.3 jit_solution(12810648757502810158)
XLA Ops:
  0.6 18.7 %shard_map.93 = (bf16[4,128,128]{2,1,0:T(8,128)(2,1)}, bf16[4,128,128]{2,1,0:T(8,128)(2,1)}, bf16[4,128,128]{2,1,0:T(8,128)(2,1)}, f32[16,128]{1,0:T(8,128)}) custom-call(bf16[4,128,128]{2,1,0:T(8,128)(2,1)} %q_hbm.1, bf16[4,128,128]{2,1,0:T(8,128)(2,1)} %k_hbm.1, bf16[4,128,128]{2,1,0:T(8,128)(2,1)} %v_hbm.1, bf16[4,128,128]{2,1,0:T(8,128)(2,1)} %g_hbm.1, ...), custom_call_target="tpu_custom_call" | custom-call | tf_op jit(solution)/shard_map/pallas_call | solution.py:143
  19.4 0.0 copy-start.1
  19.4 1.6 %copy.14 = bf16[4,128,128]{2,1,0:T(8,128)(2,1)} copy(bf16[4,128,128]{2,1,0:T(8,128)(2,1)} %get-tuple-element.16) | data formatting | bytes 262144
  21.0 0.0 copy-done.1
  21.0 0.0 copy-start
  21.0 0.7 %copy.15 = bf16[4,128,128]{2,1,0:T(8,128)(2,1)} copy(bf16[4,128,128]{2,1,0:T(8,128)(2,1)S(1)} %copy-done.1) | data formatting | bytes 262144
  21.7 0.3 %copy-done = bf16[4,128,128]{2,1,0:T(8,128)(2,1)S(1)} copy-done((bf16[4,128,128]{2,1,0:T(8,128)(2,1)S(1)}, bf16[4,128,128]{2,1,0:T(8,128)(2,1)}, u32[]{:S(2)}) %copy-start) | copy-done | bytes 131096
  22.0 0.0 copy-start.2
  22.0 0.7 %copy.16 = bf16[4,128,128]{2,1,0:T(8,128)(2,1)} copy(bf16[4,128,128]{2,1,0:T(8,128)(2,1)S(1)} %copy-done) | data formatting | bytes 262144
  22.6 0.0 copy-done.2
  22.7 0.6 %copy.17 = f32[4,4,128]{2,1,0:T(4,128)} copy(f32[4,4,128]{2,1,0:T(4,128)S(1)} %bitcast.4) | data formatting | bytes 16384
Async XLA Ops:
  19.4 1.6 %copy-start.1 = (bf16[4,128,128]{2,1,0:T(8,128)(2,1)S(1)}, bf16[4,128,128]{2,1,0:T(8,128)(2,1)}, u32[]{:S(2)}) copy-start(bf16[4,128,128]{2,1,0:T(8,128)(2,1)} %get-tuple-element.17) | copy-start | bytes 393220
  21.0 1.0 %copy-start = (bf16[4,128,128]{2,1,0:T(8,128)(2,1)S(1)}, bf16[4,128,128]{2,1,0:T(8,128)(2,1)}, u32[]{:S(2)}) copy-start(bf16[4,128,128]{2,1,0:T(8,128)(2,1)} %get-tuple-element.18) | copy-start | bytes 393220
  22.0 0.7 %copy-start.2 = (f32[16,128]{1,0:T(8,128)S(1)}, f32[16,128]{1,0:T(8,128)}, u32[]{:S(2)}) copy-start(f32[16,128]{1,0:T(8,128)} %get-tuple-element.11) | copy-start | bytes 24580

commit v2 on v1

--- a/solution.py
+++ b/solution.py
@@ -132,6 +132,16 @@
     pltpu.make_async_copy(arrived, arrived, term_send).wait()
 
 
+def write_out(*refs):
+    half = len(refs) // 2
+    sem = refs[-1]
+    copies = [pltpu.make_async_copy(refs[i], refs[half + i], sem.at[i]) for i in range(half)]
+    for copy in copies:
+        copy.start()
+    for copy in copies:
+        copy.wait()
+
+
 def local(count, queries, keys, values, grads_out, log_norm, bias):
     rows, length, channels = queries.shape
     bias_rows, heads, _ = bias.shape
@@ -140,14 +150,10 @@
     any_space = pl.BlockSpec(memory_space=pl.ANY)
     vmem = pl.BlockSpec(memory_space=pltpu.VMEM)
     big = (rows, length, channels)
+    shapes = ((big, BF16), (big, BF16), (big, BF16), ((block, length), F32))
     outs = pl.pallas_call(
         functools.partial(kernel, count, heads),
-        out_shape=(
-            jax.ShapeDtypeStruct(big, BF16),
-            jax.ShapeDtypeStruct(big, BF16),
-            jax.ShapeDtypeStruct(big, BF16),
-            jax.ShapeDtypeStruct((block, length), F32),
-        ),
+        out_shape=tuple(pltpu.VMEM(*s) for s in shapes),
         in_specs=[any_space] * 6,
         out_specs=(vmem,) * 4,
         scratch_shapes=[
@@ -179,6 +185,13 @@
         queries, keys, values, grads_out,
         log_norm.reshape(rows * heads, length), bias.reshape(block, length),
     )
+    outs = pl.pallas_call(
+        write_out,
+        out_shape=tuple(jax.ShapeDtypeStruct(*s) for s in shapes),
+        in_specs=[vmem] * 4,
+        out_specs=(any_space,) * 4,
+        scratch_shapes=[pltpu.SemaphoreType.DMA((4,))],
+    )(*(pltpu.with_memory_space_constraint(o, pltpu.VMEM) for o in outs))
     return outs[0], outs[1], outs[2], outs[3].reshape(bias_rows, heads, length)
 
 

time: 23.5 us -> 19.6 us (0.83)
  local copies, waits for them, and re-layouts: 3.85 us -> 0 us
    unnamed x10 -> x0, local copies, waits for them, and re-layouts: 3.85 us -> none
    pallas_call x1 -> x2, Pallas kernels: 18.7 us -> 18.8 us  [the longest x1 18 us: local(): pl.pallas_call(functools.partial(kernel, count, heads), out_shape=tuple((...]
where the time goes in v2:
time: 19.6 us; the launch traced here: 19.4 us
  Pallas kernels  18.8 us (96%)
  between operations  0.64 us (3%)
    pallas_call x1, Pallas kernels, local(): pl.pallas_call(functools.partial(kernel, count, heads), out_shape=tuple((...  18 us
    pallas_call x1, Pallas kernels, local(): pl.pallas_call(write_out, out_shape=tuple((jax.ShapeDtypeStruct(*s) for s...  0.78 us

profile of v2, /device:TPU:0, one launch (start us, length us, event | category | flops | bytes accessed | tf_op | source)
XLA Modules:
  0.0 19.4 jit_solution(1409500045059662644)
XLA Ops:
  0.6 18.0 %shard_map.93 = (bf16[4,128,128]{2,1,0:T(8,128)(2,1)S(1)}, bf16[4,128,128]{2,1,0:T(8,128)(2,1)S(1)}, bf16[4,128,128]{2,1,0:T(8,128)(2,1)S(1)}, f32[16,128]{1,0:T(8,128)S(1)}) custom-call(bf16[4,128,128]{2,1,0:T(8,128)(2,1)} %q_hbm.1, bf16[4,128,128]{2,1,0:T(8,128)(2,1)} %k_hbm.1, bf16[4,128,128]{2,1,0:T(8,128)(2,1)} %v_hbm.1, bf16[4,128,128]{2,1,0:T(8,128)(2,1)} %g_hbm.1, ...), custom_call_target="tpu_custom_call" | custom-call | tf_op jit(solution)/shard_map/pallas_call | solution.py:154
  18.6 0.8 %shard_map.94 = (bf16[4,128,128]{2,1,0:T(8,128)(2,1)}, bf16[4,128,128]{2,1,0:T(8,128)(2,1)}, bf16[4,128,128]{2,1,0:T(8,128)(2,1)}, f32[16,128]{1,0:T(8,128)}) custom-call(bf16[4,128,128]{2,1,0:T(8,128)(2,1)S(1)} %get-tuple-element.12.refs_0_, bf16[4,128,128]{2,1,0:T(8,128)(2,1)S(1)} %get-tuple-element.13.refs_1_, ...), custom_call_target="tpu_custom_call" | custom-call | tf_op jit(solution)/shard_map/pallas_call | solution.py:188

commit v3 on v2

--- a/solution.py
+++ b/solution.py
@@ -12,12 +12,21 @@
 BF16 = jnp.bfloat16
 
 
-def peers(me, count, body):
-    def step(d, carry):
-        body(d, lax.rem(me + d, count))
+def ascending(me, count, body):
+    def step(at, carry):
+        body(at + (at + count - me) // count)
         return carry
 
-    lax.fori_loop(1, count, step, 0)
+    lax.fori_loop(0, count - 1, step, 0)
+
+
+def descending(me, count, body):
+    def step(at, carry):
+        back = count - 2 - at
+        body(back + (back + count - me) // count)
+        return carry
+
+    lax.fori_loop(0, count - 1, step, 0)
 
 
 def kernel(
@@ -36,7 +45,7 @@
     own = pl.ds(pl.multiple_of(me * block, block), block)
 
     barrier = pltpu.get_barrier_semaphore()
-    peers(me, count, lambda d, t: pl.semaphore_signal(barrier, inc=1, device_id={"row": t}))
+    ascending(me, count, lambda t: pl.semaphore_signal(barrier, inc=1, device_id={"row": t}))
 
     pairs = ((bias_hbm, gath.at[own]), (q_hbm, q), (k_hbm, k), (v_hbm, v), (g_hbm, g), (norm_hbm, norm))
     copies = [pltpu.make_async_copy(a, b, in_sem.at[i]) for i, (a, b) in enumerate(pairs)]
@@ -51,7 +60,7 @@
             device_id={"row": t},
         )
 
-    peers(me, count, lambda d, t: gather_copy(t).start())
+    descending(me, count, lambda t: gather_copy(t).start())
 
     for copy in copies[1:]:
         copy.wait()
@@ -100,14 +109,15 @@
     for c in range(length // lanes):
         terms[:, pl.ds(c * lanes, lanes)] = wide[c].astype(BF16)
 
-    def term_copy(d, t):
+    def term_copy(t):
+        d = lax.rem(t - me + count, count)
         theirs = pl.ds(pl.multiple_of(t * block, block), block)
         return pltpu.make_async_remote_copy(
             src_ref=terms.at[theirs], dst_ref=landed.at[d], send_sem=term_send, recv_sem=term_recv,
             device_id={"row": t},
         )
 
-    peers(me, count, lambda d, t: term_copy(d, t).start())
+    ascending(me, count, lambda t: term_copy(t).start())
 
     for i in range(rows):
         key_part = jnp.dot(s_low[i], qm[i], preferred_element_type=F32)

time: 19.6 us -> 19 us (0.969)
  Pallas kernels: 18.8 us -> 18.2 us
    pallas_call x1, Pallas kernels: 18 us -> 17.4 us  [local(): pl.pallas_call(functools.partial(kernel, count, heads), out_shape=tuple((...]
where the time goes in v3:
time: 19 us; the launch traced here: 18.8 us
  Pallas kernels  18.2 us (96%)
  between operations  0.64 us (3%)
    pallas_call x1, Pallas kernels, local(): pl.pallas_call(functools.partial(kernel, count, heads), out_shape=tuple((...  17.4 us
    pallas_call x1, Pallas kernels, local(): pl.pallas_call(write_out, out_shape=tuple((jax.ShapeDtypeStruct(*s) for s...  0.78 us

profile of v3, /device:TPU:0, one launch (start us, length us, event | category | flops | bytes accessed | tf_op | source)
XLA Modules:
  0.0 18.8 jit_solution(16058173344170124394)
XLA Ops:
  0.6 17.4 %shard_map.93 = (bf16[4,128,128]{2,1,0:T(8,128)(2,1)S(1)}, bf16[4,128,128]{2,1,0:T(8,128)(2,1)S(1)}, bf16[4,128,128]{2,1,0:T(8,128)(2,1)S(1)}, f32[16,128]{1,0:T(8,128)S(1)}) custom-call(bf16[4,128,128]{2,1,0:T(8,128)(2,1)} %q_hbm.1, bf16[4,128,128]{2,1,0:T(8,128)(2,1)} %k_hbm.1, bf16[4,128,128]{2,1,0:T(8,128)(2,1)} %v_hbm.1, bf16[4,128,128]{2,1,0:T(8,128)(2,1)} %g_hbm.1, ...), custom_call_target="tpu_custom_call" | custom-call | tf_op jit(solution)/shard_map/pallas_call | solution.py:164
  18.0 0.8 %shard_map.94 = (bf16[4,128,128]{2,1,0:T(8,128)(2,1)}, bf16[4,128,128]{2,1,0:T(8,128)(2,1)}, bf16[4,128,128]{2,1,0:T(8,128)(2,1)}, f32[16,128]{1,0:T(8,128)}) custom-call(bf16[4,128,128]{2,1,0:T(8,128)(2,1)S(1)} %get-tuple-element.12.refs_0_, bf16[4,128,128]{2,1,0:T(8,128)(2,1)S(1)} %get-tuple-element.13.refs_1_, ...), custom_call_target="tpu_custom_call" | custom-call | tf_op jit(solution)/shard_map/pallas_call | solution.py:198

commit v4 on v3

--- a/solution.py
+++ b/solution.py
@@ -20,13 +20,19 @@
     lax.fori_loop(0, count - 1, step, 0)
 
 
-def descending(me, count, body):
+def outside_in(me, count, low_first, body):
     def step(at, carry):
-        back = count - 2 - at
-        body(back + (back + count - me) // count)
+        side = lax.rem(at + low_first, 2)
+        near = lax.div(at, 2)
+        target = side * near + (1 - side) * (count - 1 - near)
+
+        @pl.when(target != me)
+        def _():
+            body(target)
+
         return carry
 
-    lax.fori_loop(0, count - 1, step, 0)
+    lax.fori_loop(0, count, step, 0)
 
 
 def kernel(
@@ -60,7 +66,7 @@
             device_id={"row": t},
         )
 
-    descending(me, count, lambda t: gather_copy(t).start())
+    outside_in(me, count, 0, lambda t: gather_copy(t).start())
 
     for copy in copies[1:]:
         copy.wait()
@@ -117,7 +123,7 @@
             device_id={"row": t},
         )
 
-    ascending(me, count, lambda t: term_copy(t).start())
+    outside_in(me, count, 1, lambda t: term_copy(t).start())
 
     for i in range(rows):
         key_part = jnp.dot(s_low[i], qm[i], preferred_element_type=F32)

time: 19 us -> 18.2 us (0.958)
  Pallas kernels: 18.2 us -> 17.4 us
    pallas_call x1, Pallas kernels: 17.4 us -> 16.6 us  [local(): pl.pallas_call(functools.partial(kernel, count, heads), out_shape=tuple((...]
where the time goes in v4:
time: 18.2 us; the launch traced here: 18 us
  Pallas kernels  17.4 us (96%)
  between operations  0.64 us (4%)
    pallas_call x1, Pallas kernels, local(): pl.pallas_call(functools.partial(kernel, count, heads), out_shape=tuple((...  16.6 us
    pallas_call x1, Pallas kernels, local(): pl.pallas_call(write_out, out_shape=tuple((jax.ShapeDtypeStruct(*s) for s...  0.78 us

profile of v4, /device:TPU:0, one launch (start us, length us, event | category | flops | bytes accessed | tf_op | source)
XLA Modules:
  0.0 18.0 jit_solution(5313356757126963927)
XLA Ops:
  0.6 16.6 %shard_map.93 = (bf16[4,128,128]{2,1,0:T(8,128)(2,1)S(1)}, bf16[4,128,128]{2,1,0:T(8,128)(2,1)S(1)}, bf16[4,128,128]{2,1,0:T(8,128)(2,1)S(1)}, f32[16,128]{1,0:T(8,128)S(1)}) custom-call(bf16[4,128,128]{2,1,0:T(8,128)(2,1)} %q_hbm.1, bf16[4,128,128]{2,1,0:T(8,128)(2,1)} %k_hbm.1, bf16[4,128,128]{2,1,0:T(8,128)(2,1)} %v_hbm.1, bf16[4,128,128]{2,1,0:T(8,128)(2,1)} %g_hbm.1, ...), custom_call_target="tpu_custom_call" | custom-call | tf_op jit(solution)/shard_map/pallas_call | solution.py:170
  17.3 0.8 %shard_map.94 = (bf16[4,128,128]{2,1,0:T(8,128)(2,1)}, bf16[4,128,128]{2,1,0:T(8,128)(2,1)}, bf16[4,128,128]{2,1,0:T(8,128)(2,1)}, f32[16,128]{1,0:T(8,128)}) custom-call(bf16[4,128,128]{2,1,0:T(8,128)(2,1)S(1)} %get-tuple-element.12.refs_0_, bf16[4,128,128]{2,1,0:T(8,128)(2,1)S(1)} %get-tuple-element.13.refs_1_, ...), custom_call_target="tpu_custom_call" | custom-call | tf_op jit(solution)/shard_map/pallas_call | solution.py:204
